TPU v7x, 32 devices: a 4x4x1 block of a 4x4x8 slice. The times are simulated.
32 devices in a mesh: stage: 1 (over z), data: 32 (over y, x, core).
Axes of the slice: x: 4, y: 4, z: 1, core: 2. Of those that a mesh axis runs over, the one named last changes fastest.
The devices are a block of a 4x4x8 slice.
Arguments:
- w_master: float32 [64, 512, 512], P('stage', 'data')
- momentum: float32 [64, 512, 512], P('stage', 'data')
- grads: bfloat16 [32, 64, 512, 512], P(('stage', 'data'))
Outputs:
- output 1: float32 [64, 512, 512], P('stage', 'data')
- output 2: float32 [64, 512, 512], P('stage', 'data')
All inputs are finite; a program needn't handle non-finite values.
Results may differ from a plain program's by a relative error of at most 0.0147319.
Values are sent between devices in bfloat16 or wider.
A program may use at most 768 MiB of HBM per device.

v0:
```python
import math
import jax
import jax.numpy as jnp
from jax import lax
from jax.sharding import PartitionSpec as P, NamedSharding

MOMENTUM_COEF = 0.95
LEARN_RATE = 0.05
WEIGHT_DECAY = 0.2
NORM_EPS = 1e-7
COEF_A = 3.4445
COEF_B = -4.7750
COEF_C = 2.0315
NS_ITERS = 5


def newton_schulz(x_cur):
    n_rows, n_cols = x_cur.shape[1], x_cur.shape[2]
    for _ in range(NS_ITERS):
        if n_rows > n_cols:
            gram_f = jnp.einsum('bri,brj->bij', x_cur, x_cur, preferred_element_type=jnp.float32)
        else:
            gram_f = jnp.einsum('bik,bjk->bij', x_cur, x_cur, preferred_element_type=jnp.float32)
        gram_mat = gram_f.astype(jnp.bfloat16)
        gram_sq = jnp.einsum('bij,bjk->bik', gram_mat, gram_mat, preferred_element_type=jnp.float32)
        poly_mat = (COEF_B * gram_mat.astype(jnp.float32) + COEF_C * gram_sq).astype(jnp.bfloat16)
        if n_rows > n_cols:
            poly_x = jnp.einsum('brj,bij->bri', x_cur, poly_mat, preferred_element_type=jnp.float32)
        else:
            poly_x = jnp.einsum('bij,bjk->bik', poly_mat, x_cur, preferred_element_type=jnp.float32)
        x_cur = (COEF_A * x_cur.astype(jnp.float32) + poly_x).astype(jnp.bfloat16)
    return x_cur


def solution(mesh):
    group_size = mesh.shape['data']
    row_spec = P('stage', 'data', None)
    grad_spec = P(('stage', 'data'), None, None, None)

    def local_step(w_rows, mom_rows, grad_full):
        n_mats, rows_dev, n_cols = w_rows.shape
        n_rows = rows_dev * group_size
        per_dev = n_mats // group_size
        my_index = lax.axis_index('data')
        grad_rows = lax.psum_scatter(grad_full[0].astype(jnp.float32), 'data', scatter_dimension=1, tiled=True)
        mom_new = MOMENTUM_COEF * mom_rows + grad_rows
        frob_norm = jnp.sqrt(lax.psum(jnp.sum(mom_new * mom_new, axis=(1, 2)), 'data'))
        owned_mom = lax.all_to_all(mom_new.astype(jnp.bfloat16), 'data', 0, 1, tiled=True)
        owned_norm = lax.dynamic_slice_in_dim(frob_norm, my_index * per_dev, per_dev)
        x_start = (owned_mom.astype(jnp.float32) / (owned_norm[:, None, None] + NORM_EPS)).astype(jnp.bfloat16)
        x_ortho = newton_schulz(x_start)
        x_rows = lax.all_to_all(x_ortho, 'data', 1, 0, tiled=True)
        rms_scale = 0.2 * math.sqrt(max(n_rows, n_cols))
        w_new = w_rows - LEARN_RATE * (x_rows.astype(jnp.float32) * rms_scale + WEIGHT_DECAY * w_rows)
        return w_new, mom_new

    return jax.shard_map(local_step, mesh=mesh, in_specs=(row_spec, row_spec, grad_spec), out_specs=(row_spec, row_spec), check_vma=False)
```

profile of v0, /device:TPU:97, one launch (start us, length us, event | category | flops | bytes accessed | tf_op | source)
XLA Modules:
  0.0 434.6 jit_solution(6628498498470767833)
XLA Ops:
  7.2 32.4 %bitcast_convert_fusion = f32[64,512,512]{2,1,0:T(8,128)} fusion(bf16[1,64,512,512]{3,2,1,0:T(8,128)(2,1)} %param.5), kind=kLoop, calls=%fused_computation | loop fusion | flops 16777216 | bytes 100663296 | tf_op jit(solution)/shard_map/convert_element_type | solution.py:45
  39.7 288.3 %reduce-scatter.2.cloned.1.call-done = f32[64,16,512]{2,1,0:T(8,128)} async-done(((f32[64,512,512]{2,1,0:T(8,128)}), f32[64,16,512]{2,1,0:T(8,128)}) %reduce-scatter.2.cloned.1.call-update) | async-done | bytes 2097168 | tf_op jit(solution)/shard_map/reduce_scatter | solution.py:45
  328.1 2.8 multiply_reduce_fusion
  330.8 1.3 convert_element_type.107
  332.1 0.4 copy-done
  332.5 5.2 %all-to-all-start = ((bf16[64,16,512]{2,1,0:T(8,128)(2,1)}), bf16[64,16,512]{2,1,0:T(8,128)(2,1)S(1)}, u32[]{:S(2)}, u32[]{:S(2)}) async-start(bf16[64,16,512]{2,1,0:T(8,128)(2,1)} %convert_element_type.107), calls=%async_computation.1 | async-start | bytes 2097152 | tf_op jit(solution)/shard_map/all_to_all | solution.py:48
  337.7 53.2 %psum.7 = f32[64]{0:T(128)S(1)} all-reduce(f32[64]{0:T(128)S(1)} %get-tuple-element.2), channel_id=1, replica_groups=mesh['stage'=1,'data'=32] {'data'}, use_global_device_ids=true, to_apply=%region_2.0 | all-reduce | flops 64 | bytes 512 | tf_op jit(solution)/shard_map/psum | solution.py:47
  391.2 0.3 fusion
  391.6 0.7 convolution_convert_fusion.4
  392.3 1.3 add_convert_fusion.8
  393.6 0.7 convolution_convert_fusion.3
  394.4 1.3 add_convert_fusion.6
  395.7 0.7 convolution_convert_fusion.2
  396.4 1.3 add_convert_fusion.4
  397.7 0.7 convolution_convert_fusion.1
  398.4 1.3 add_convert_fusion.2
  399.7 0.7 convolution_convert_fusion
  400.5 1.3 add_convert_fusion
  401.8 1.1 copy.8
  402.9 20.3 %all_to_all.8 = bf16[2,512,512]{2,0,1:T(2,128)(2,1)S(1)} all-to-all(bf16[2,512,512]{2,0,1:T(2,128)(2,1)S(1)} %copy.8), channel_id=1, replica_groups=mesh['stage'=1,'data'=32] {'data'}, dimensions={1} | all-to-all | bytes 2097152 | tf_op jit(solution)/shard_map/all_to_all | solution.py:52
  423.2 1.1 convert_multiply_fusion
  424.3 0.4 copy.9
  424.7 1.2 copy-done.1
  425.9 1.8 fusion.2
  (8 shorter events, 0.5 us)
Async XLA Ops:
  7.2 320.9 %reduce-scatter.2.cloned.1.call-start = ((), (), s32[]{:S(2)}) async-start(), calls=%async_computation.3 | async-start | bytes 69206016 | tf_op jit(solution)/shard_map/reduce_scatter | solution.py:45
  330.8 1.7 copy-start
  332.5 58.4 %all-to-all-start = ((bf16[64,16,512]{2,1,0:T(8,128)(2,1)}), bf16[64,16,512]{2,1,0:T(8,128)(2,1)S(1)}, u32[]{:S(2)}, u32[]{:S(2)}) async-start(bf16[64,16,512]{2,1,0:T(8,128)(2,1)} %convert_element_type.107), calls=%async_computation.1 | async-start | bytes 2097152 | tf_op jit(solution)/shard_map/all_to_all | solution.py:48
  424.3 1.6 copy-start.1
Sparse Core Ops, SparseCore 0:
  39.8 288.1 reduce-scatter.1
where the time goes:
time: 435 us
  waiting for transfers between devices  288 us (66%)
  blocking collectives  73.5 us (17%)
  other arithmetic  39.8 us (9%)
  between operations  14.2 us (3%)
  matrix products  10.1 us (2%)
  starting transfers between devices  5.22 us (1%)
    reduce_scatter x1, waiting for transfers between devices, local_step(): lax.psum_scatter(grad_full[0].astype(jnp.float32), 'data', scatter_dimens...  288 us
    psum x1, blocking collectives, local_step(): lax.psum(jnp.sum(mom_new * mom_new, axis=(1, 2)), 'data')  53.2 us
    convert_element_type x1, other arithmetic, local_step(): grad_full[0].astype(jnp.float32)  32.4 us
    all_to_all x1, blocking collectives, local_step(): x_rows = lax.all_to_all(x_ortho, 'data', 1, 0, tiled=True)  20.3 us
  transfers between devices with their start and end apart: 2, of which 1 were waited for; matrix products, arithmetic and copies ran while one was open for 0% of the time, Pallas kernels for 0%

commit v1 on v0

v1 whole, which is shorter than its diff:
```python
import functools
import math

import jax
import jax.numpy as jnp
from jax import lax
from jax.experimental import pallas as pl
from jax.experimental.pallas import tpu as pltpu
from jax.sharding import PartitionSpec as P

MOMENTUM_COEF = 0.95
LEARN_RATE = 0.05
WEIGHT_DECAY = 0.2
NORM_EPS = 1e-7
COEF_A = 3.4445
COEF_B = -4.7750
COEF_C = 2.0315
NS_ITERS = 5

CORES = 2
RING = 4
SIGNS = (1, -1, 1, -1)
X_FIRST = (True, True, False, False)
GROUPS = 4
PER_GROUP = 1
IN_SLOTS = 6
SEND_SLOTS = 3
AHEAD = 2
MESH = pl.DeviceIdType.MESH


def _kernel(
    devs, grads, mom_in, mom_out, rows_out,
    own, peer, r1, r2, r3, p1, p2, p3, lead, mom, half_out, sq_out, half_in, sq_in, x_buf, gram, poly,
    own_sem, peer_send, peer_recv, peer_free, lead_send, r_recv, fwd_send, p_recv, part_send, last_send,
    mom_sem, mom_done, half_send, sq_send, half_recv, sq_recv, x_send, x_recv, x_self,
):
    n_mats, rows, cols = mom.shape
    q = PER_GROUP
    m = GROUPS * q
    chunks = n_mats // m
    slots = n_mats // devs
    f32, bf16 = jnp.float32, jnp.bfloat16

    me = lax.axis_index('data')
    core = lax.rem(me, CORES)
    chip = me // CORES
    px, py = lax.rem(chip, RING), chip // RING
    buddy = me + 1 - 2 * core

    def at(pos, step):
        return lax.rem(pos + step + RING, RING)

    def device(x, y):
        return (y * RING + x) * CORES + core

    def first(g):
        return px if X_FIRST[g] else py

    def second(g):
        return py if X_FIRST[g] else px

    def chip_of(g, on_first, on_second):
        x, y = (on_first, on_second) if X_FIRST[g] else (on_second, on_first)
        return y * RING + x

    def near_first(g, step):
        return device(at(px, step), py) if X_FIRST[g] else device(px, at(py, step))

    def near_second(g, step):
        return device(px, at(py, step)) if X_FIRST[g] else device(at(px, step), py)

    def remote(src, dst, send, recv, target):
        return pltpu.make_async_remote_copy(
            src_ref=src, dst_ref=dst, send_sem=send, recv_sem=recv,
            device_id={'data': target}, device_id_type=MESH)

    def wait_bytes(ref, sem):
        pltpu.make_async_copy(ref, ref, sem).wait()

    def owner_of(j):
        jj = lax.rem(j, devs)
        return lax.rem(jj, RING) * (devs // RING) + jj // RING

    barrier = pltpu.get_barrier_semaphore()

    @pl.loop(1, devs)
    def _(i):
        pl.semaphore_signal(barrier, inc=1, device_id={'data': lax.rem(me + i, devs)}, device_id_type=MESH)

    pl.semaphore_wait(barrier, devs - 1)

    def fetch(k):
        slot = lax.rem(k, IN_SLOTS)
        pltpu.make_async_copy(grads.at[pl.ds(k * m, m), :, core], own.at[slot], own_sem.at[slot]).start()

        @pl.when(k >= IN_SLOTS)
        def _():
            pl.semaphore_wait(peer_free, 1)

        remote(grads.at[pl.ds(k * m, m), :, 1 - core], peer.at[slot], peer_send.at[slot], peer_recv.at[slot], buddy).start()

    def pair(slot, g, i, on_first, o):
        c = chip_of(g, on_first, o)
        return own[slot, g * q + i, c].astype(f32) + peer[slot, g * q + i, c].astype(f32)

    def lead_stage(k):
        slot, st = lax.rem(k, IN_SLOTS), lax.rem(k, SEND_SLOTS)
        wait_bytes(own.at[slot], own_sem.at[slot])
        wait_bytes(peer.at[slot], peer_send.at[slot])
        wait_bytes(peer.at[slot], peer_recv.at[slot])

        @pl.when(k >= SEND_SLOTS)
        def _():
            wait_bytes(lead.at[st], lead_send.at[st])

        for role, step in ((0, 2), (1, -1)):
            for g in range(GROUPS):
                dest = at(first(g), step * SIGNS[g])
                for o in range(RING):
                    for i in range(q):
                        lead[st, role, g, o, i] = pair(slot, g, i, dest, o)
        for g in range(GROUPS):
            remote(lead.at[st, 0, g], r1.at[k, g], lead_send.at[st], r_recv.at[0, k], near_first(g, SIGNS[g])).start()
            remote(lead.at[st, 1, g], r2.at[k, g], lead_send.at[st], r_recv.at[1, k], near_first(g, -SIGNS[g])).start()

    def forward_stage(k):
        slot = lax.rem(k, IN_SLOTS)
        wait_bytes(r1.at[k], r_recv.at[0, k])
        for g in range(GROUPS):
            dest = at(first(g), SIGNS[g])
            for o in range(RING):
                for i in range(q):
                    r1[k, g, o, i] = r1[k, g, o, i] + pair(slot, g, i, dest, o)
        for g in range(GROUPS):
            remote(r1.at[k, g], r3.at[k, g], fwd_send.at[k], r_recv.at[2, k], near_first(g, SIGNS[g])).start()

    def part_stage(k):
        slot = lax.rem(k, IN_SLOTS)
        wait_bytes(r2.at[k], r_recv.at[1, k])
        wait_bytes(r3.at[k], r_recv.at[2, k])
        for g in range(GROUPS):
            for o in range(RING):
                for i in range(q):
                    r3[k, g, o, i] = (r3[k, g, o, i] + r2[k, g, o, i]) + pair(slot, g, i, first(g), o)

        @pl.when(k + IN_SLOTS < chunks)
        def _():
            pl.semaphore_signal(peer_free, inc=1, device_id={'data': buddy}, device_id_type=MESH)

        for g in range(GROUPS):
            s = SIGNS[g]
            remote(r3.at[k, g, at(second(g), 2 * s)], p1.at[k, g], part_send.at[k], p_recv.at[0, k], near_second(g, s)).start()
            remote(r3.at[k, g, at(second(g), -s)], p2.at[k, g], part_send.at[k], p_recv.at[1, k], near_second(g, -s)).start()

    def last_stage(k):
        wait_bytes(p1.at[k], p_recv.at[0, k])
        for g in range(GROUPS):
            dest = at(second(g), SIGNS[g])
            for i in range(q):
                p1[k, g, i] = p1[k, g, i] + r3[k, g, dest, i]
        for g in range(GROUPS):
            remote(p1.at[k, g], p3.at[k, g], last_send.at[k], p_recv.at[2, k], near_second(g, SIGNS[g])).start()

    def final_stage(k):
        @pl.when(k == 0)
        def _():
            wait_bytes(mom, mom_sem)

        wait_bytes(p2.at[k], p_recv.at[1, k])
        wait_bytes(p3.at[k], p_recv.at[2, k])
        for g in range(GROUPS):
            for i in range(q):
                j = k * m + g * q + i
                total = r3[k, g, second(g), i] + p2[k, g, i] + p3[k, g, i]
                new = MOMENTUM_COEF * mom[j] + total
                mom[j] = new
                short = new.astype(bf16)
                sq = jnp.sum(new * new, axis=0, keepdims=True)
                sq = functools.reduce(jnp.add, [sq[:, n * 128:(n + 1) * 128] for n in range(cols // 128)])
                half_out[j] = short
                sq_out[j] = sq
                owner, slot = owner_of(j), j // devs

                @pl.when(owner == me)
                def _():
                    half_in[slot, me] = short
                    sq_in[slot, me] = sq

        pltpu.make_async_copy(mom.at[pl.ds(k * m, m)], mom_out.at[pl.ds(k * m, m)], mom_done).start()

        for n in range(m):
            j = k * m + n
            owner, slot = owner_of(j), j // devs

            @pl.when(owner != me)
            def _():
                remote(half_out.at[j], half_in.at[slot, me], half_send, half_recv.at[slot], owner).start()
                remote(sq_out.at[j], sq_in.at[slot, me], sq_send, sq_recv.at[slot], owner).start()

    def ns_start(slot):
        wait_bytes(half_in.at[slot, pl.ds(0, devs - 1)], half_recv.at[slot])
        wait_bytes(sq_in.at[slot, pl.ds(0, devs - 1)], sq_recv.at[slot])
        sq = jnp.sum(jnp.sum(sq_in[slot], axis=0), axis=1, keepdims=True)
        scale = jnp.sqrt(sq) + NORM_EPS

        @pl.loop(0, devs)
        def _(d):
            x_buf[slot, pl.ds(pl.multiple_of(d * rows, rows), rows), :] = (half_in[slot, d].astype(f32) / scale).astype(bf16)

    def ns_iter(slot):
        x = x_buf[slot]
        gram[...] = lax.dot_general(x, x, (((1,), (1,)), ((), ())), preferred_element_type=f32).astype(bf16)
        a = gram[...]
        poly[...] = (COEF_B * a.astype(f32) + COEF_C * jnp.dot(a, a, preferred_element_type=f32)).astype(bf16)
        x_buf[slot] = (COEF_A * x.astype(f32) + jnp.dot(poly[...], x, preferred_element_type=f32)).astype(bf16)

    def mat_of(slot, d):
        return slot * devs + lax.rem(d, devs // RING) * RING + d // (devs // RING)

    def x_block(slot, d):
        return x_buf.at[slot, pl.ds(pl.multiple_of(d * rows, rows), rows), :]

    def x_give(slot):
        j = mat_of(slot, me)

        @pl.loop(1, devs)
        def _(i):
            d = lax.rem(me + i, devs)
            remote(x_block(slot, d), rows_out.at[j], x_send.at[slot], x_recv.at[slot], d).start()

        pltpu.make_async_copy(x_block(slot, me), rows_out.at[j], x_self.at[slot]).start()

    pltpu.make_async_copy(mom_in, mom, mom_sem).start()
    for k in range(AHEAD):
        fetch(jnp.int32(k))

    ns_at = chunks // slots + 4
    steps = max(chunks + 4, ns_at + NS_ITERS)

    @pl.loop(0, steps)
    def _(t):
        @pl.when(t + AHEAD < chunks)
        def _():
            fetch(t + AHEAD)

        for lag, stage in enumerate((lead_stage, forward_stage, part_stage, last_stage, final_stage)):
            @pl.when(jnp.logical_and(t >= lag, t < chunks + lag))
            def _():
                stage(t - lag)

        @pl.when(t == ns_at)
        def _():
            ns_start(0)

        @pl.when(jnp.logical_and(t >= ns_at, t < ns_at + NS_ITERS))
        def _():
            ns_iter(0)

        @pl.when(t == ns_at + NS_ITERS - 1)
        def _():
            x_give(0)

    for slot in range(1, slots):
        ns_start(slot)

        @pl.loop(0, NS_ITERS)
        def _(i):
            ns_iter(slot)

        x_give(slot)

    @pl.loop(0, chunks)
    def _(k):
        wait_bytes(r1.at[k], fwd_send.at[k])
        wait_bytes(p1.at[k], part_send.at[k])
        wait_bytes(p2.at[k], part_send.at[k])
        wait_bytes(p1.at[k], last_send.at[k])

    for st in range(SEND_SLOTS):
        wait_bytes(lead.at[st], lead_send.at[st])
    wait_bytes(mom, mom_done)
    wait_bytes(half_out.at[pl.ds(0, n_mats - slots)], half_send)
    wait_bytes(sq_out.at[pl.ds(0, n_mats - slots)], sq_send)
    for slot in range(slots):
        wait_bytes(half_in.at[slot, pl.ds(0, devs - 1)], x_send.at[slot])
        wait_bytes(half_in.at[slot, pl.ds(0, devs - 1)], x_recv.at[slot])
        pltpu.make_async_copy(x_block(slot, 0), rows_out.at[0], x_self.at[slot]).wait()


def exchange(devs, grads, mom):
    n_mats, rows, cols = mom.shape
    n_rows = rows * devs
    chips = devs // CORES
    q = PER_GROUP
    m = GROUPS * q
    chunks = n_mats // m
    slots = n_mats // devs
    f32, bf16 = jnp.float32, jnp.bfloat16
    dma, vmem = pltpu.SemaphoreType.DMA, pltpu.VMEM
    grads = grads.reshape(n_mats, chips, CORES, rows, cols)
    wide = (chunks, GROUPS, RING, q, rows, cols)
    thin = (chunks, GROUPS, q, rows, cols)
    return pl.pallas_call(
        functools.partial(_kernel, devs),
        out_shape=(
            jax.ShapeDtypeStruct(mom.shape, f32),
            jax.ShapeDtypeStruct(mom.shape, bf16),
        ),
        in_specs=[pl.BlockSpec(memory_space=pl.ANY)] * 2,
        out_specs=(pl.BlockSpec(memory_space=pl.ANY),) * 2,
        scratch_shapes=[
            vmem((IN_SLOTS, m, chips, rows, cols), bf16),
            vmem((IN_SLOTS, m, chips, rows, cols), bf16),
            vmem(wide, f32), vmem(wide, f32), vmem(wide, f32),
            vmem(thin, f32), vmem(thin, f32), vmem(thin, f32),
            vmem((SEND_SLOTS, 2, GROUPS, RING, q, rows, cols), f32),
            vmem(mom.shape, f32),
            vmem(mom.shape, bf16),
            vmem((n_mats, 1, 128), f32),
            vmem((slots, devs, rows, cols), bf16),
            vmem((slots, devs, 1, 128), f32),
            vmem((slots, n_rows, cols), bf16),
            vmem((n_rows, n_rows), bf16),
            vmem((n_rows, n_rows), bf16),
            dma((IN_SLOTS,)), dma((IN_SLOTS,)), dma((IN_SLOTS,)), pltpu.SemaphoreType.REGULAR,
            dma((SEND_SLOTS,)), dma((3, chunks)), dma((chunks,)), dma((3, chunks)), dma((chunks,)), dma((chunks,)),
            dma, dma, dma, dma, dma((slots,)), dma((slots,)), dma((slots,)), dma((slots,)), dma((slots,)),
        ],
        compiler_params=pltpu.CompilerParams(
            collective_id=0, has_side_effects=True, vmem_limit_bytes=67043328),
    )(grads, mom)


def solution(mesh):
    devs = mesh.shape['data']
    row_spec = P('stage', 'data', None)
    grad_spec = P(('stage', 'data'), None, None, None)

    def local_step(w_rows, mom_rows, grad_full):
        n_mats, rows_dev, n_cols = w_rows.shape
        n_rows = rows_dev * devs
        assert devs == RING * RING * CORES and n_rows <= n_cols
        mom_new, x_rows = exchange(devs, grad_full[0], mom_rows)
        rms_scale = 0.2 * math.sqrt(max(n_rows, n_cols))
        w_new = w_rows - LEARN_RATE * (x_rows.astype(jnp.float32) * rms_scale + WEIGHT_DECAY * w_rows)
        return w_new, mom_new

    return jax.shard_map(local_step, mesh=mesh, in_specs=(row_spec, row_spec, grad_spec), out_specs=(row_spec, row_spec), check_vma=False)
```

time: 435 us -> 228 us (0.52)
  waiting for transfers between devices: 288 us -> 0 us
  Pallas kernels: 0 us -> 222 us
  blocking collectives: 73.5 us -> 0 us
  other arithmetic: 39.8 us -> 3.86 us
  between operations: 14.2 us -> 0.65 us
  matrix products: 10.1 us -> 0 us
  starting transfers between devices: 5.22 us -> 0 us
    reduce_scatter x1 -> x0, waiting for transfers between devices: 288 us -> none  [local_step(): lax.psum_scatter(grad_full[0].astype(jnp.float32), 'data', scatter_dimens...]
    pallas_call x0 -> x1, Pallas kernels: none -> 222 us  [exchange(): pl.pallas_call(functools.partial(_kernel, devs), out_shape=(jax.ShapeDtyp...]
    psum x1 -> x0, blocking collectives: 53.2 us -> none  [local_step(): lax.psum(jnp.sum(mom_new * mom_new, axis=(1, 2)), 'data')]
    convert_element_type x3 -> x0, other arithmetic: 34 us -> none  [the longest x1 32.4 us: local_step(): grad_full[0].astype(jnp.float32)]
    all_to_all x1 -> x0, blocking collectives: 20.3 us -> none  [local_step(): x_rows = lax.all_to_all(x_ortho, 'data', 1, 0, tiled=True)]
    dot_general x10 -> x0, matrix products: 10.1 us -> none  [the longest x5 6.42 us: newton_schulz(): jnp.einsum('bij,bjk->bik', poly_mat, x_cur, preferred_element_type=jnp.fl...]
    all_to_all x1 -> x0, starting transfers between devices: 5.16 us -> none  [local_step(): lax.all_to_all(mom_new.astype(jnp.bfloat16), 'data', 0, 1, tiled=True)]
  transfers between devices with their start and end apart: 2 -> 0, of which waited for: 1 -> 0; matrix products, arithmetic and copies ran while one was open for 0% -> 0% of each run, Pallas kernels for 0% -> 0%
where the time goes in v1:
time: 228 us
  Pallas kernels  222 us (97%)
  other arithmetic  3.86 us (2%)
    pallas_call x1, Pallas kernels, exchange(): pl.pallas_call(functools.partial(_kernel, devs), out_shape=(jax.ShapeDtyp...  222 us

profile of v1, /device:TPU:97, one launch (start us, length us, event | category | flops | bytes accessed | tf_op | source)
XLA Modules:
  0.0 227.6 jit_solution(6777221613906887642)
XLA Ops:
  0.6 221.8 %shard_map.50 = (f32[64,16,512]{2,1,0:T(8,128)}, bf16[64,16,512]{2,1,0:T(8,128)(2,1)}) custom-call(bf16[64,16,2,16,512]{4,3,2,1,0:T(8,128)(2,1)} %bitcast.1, f32[64,16,512]{2,1,0:T(8,128)} %mom_in.1), custom_call_target="tpu_custom_call" | custom-call | tf_op jit(solution)/shard_map/pallas_call | solution.py:304
  222.4 0.0 copy-start
  222.4 3.9 %multiply_subtract_fusion = f32[64,16,512]{2,1,0:T(8,128)} fusion(f32[64,16,512]{2,1,0:T(8,128)} %param.3, bf16[64,16,512]{2,1,0:T(8,128)(2,1)} %get-tuple-element.4), kind=kLoop, calls=%fused_computation | loop fusion | flops 3145728 | bytes 5242880 | tf_op jit(solution)/shard_map/sub | solution.py:346
  226.3 0.0 copy-done
  226.3 1.3 copy.6
Async XLA Ops:
  222.4 3.9 %copy-start = (f32[64,16,512]{2,1,0:T(8,128)S(1)}, f32[64,16,512]{2,1,0:T(8,128)}, u32[]{:S(2)}) copy-start(f32[64,16,512]{2,1,0:T(8,128)} %get-tuple-element.9) | copy-start | bytes 6291460

commit v2 on v1

v2 whole, which is shorter than its diff:
```python
import functools
import math

import jax
import jax.numpy as jnp
from jax import lax
from jax.experimental import pallas as pl
from jax.experimental.pallas import tpu as pltpu
from jax.sharding import PartitionSpec as P

MOMENTUM_COEF = 0.95
LEARN_RATE = 0.05
WEIGHT_DECAY = 0.2
NORM_EPS = 1e-7
COEF_A = 3.4445
COEF_B = -4.7750
COEF_C = 2.0315
NS_ITERS = 5

CORES = 2
RING = 4
SIGNS = (1, -1, 1, -1)
X_FIRST = (True, True, False, False)
GROUPS = 4
IN_SLOTS = 6
SEND_SLOTS = 3
AHEAD = 2
MESH = pl.DeviceIdType.MESH


def _kernel(
    devs, grads, mom_in, w_in, mom_out, w_out,
    own, peer, r1, r2, r3, p1, p2, p3, lead, mom, w, half_out, sq_out, half_in, sq_in, x_buf, x_in, gram, poly,
    own_sem, peer_send, peer_recv, peer_free, lead_send, r_recv, fwd_send, p_recv, part_send, last_send,
    mom_sem, mom_done, w_sem, w_done, half_send, sq_send, half_recv, sq_recv, x_send, x_recv0, x_recv,
):
    n_mats, rows, cols = mom.shape
    m = GROUPS
    chunks = n_mats // m
    slots = n_mats // devs
    per_slot = chunks // slots
    rms_scale = 0.2 * math.sqrt(max(rows * devs, cols))
    f32, bf16 = jnp.float32, jnp.bfloat16

    me = lax.axis_index('data')
    core = lax.rem(me, CORES)
    chip = me // CORES
    px, py = lax.rem(chip, RING), chip // RING
    buddy = me + 1 - 2 * core

    def at(pos, step):
        return lax.rem(pos + step + RING, RING)

    def device(x, y):
        return (y * RING + x) * CORES + core

    def first(g):
        return px if X_FIRST[g] else py

    def second(g):
        return py if X_FIRST[g] else px

    def chip_of(g, on_first, on_second):
        x, y = (on_first, on_second) if X_FIRST[g] else (on_second, on_first)
        return y * RING + x

    def near_first(g, step):
        return device(at(px, step), py) if X_FIRST[g] else device(px, at(py, step))

    def near_second(g, step):
        return device(px, at(py, step)) if X_FIRST[g] else device(at(px, step), py)

    def remote(src, dst, send, recv, target):
        return pltpu.make_async_remote_copy(
            src_ref=src, dst_ref=dst, send_sem=send, recv_sem=recv,
            device_id={'data': target}, device_id_type=MESH)

    def wait_bytes(ref, sem):
        pltpu.make_async_copy(ref, ref, sem).wait()

    def owner_of(k, g):
        kk = lax.rem(k, per_slot)
        return (g * RING + lax.rem(kk + g, RING)) * CORES + kk // RING

    my_turn = RING * core + at(px, -py)

    def mine(slot):
        return (slot * per_slot + my_turn) * m + py

    def fetch_own(k):
        slot = lax.rem(k, IN_SLOTS)
        pltpu.make_async_copy(grads.at[pl.ds(k * m, m), :, core], own.at[slot], own_sem.at[slot]).start()

    def fetch_peer(k):
        slot = lax.rem(k, IN_SLOTS)

        @pl.when(k >= IN_SLOTS)
        def _():
            pl.semaphore_wait(peer_free, 1)

        remote(grads.at[pl.ds(k * m, m), :, 1 - core], peer.at[slot], peer_send.at[slot], peer_recv.at[slot], buddy).start()

    def pair(slot, g, on_first, o):
        c = chip_of(g, on_first, o)
        return own[slot, g, c].astype(f32) + peer[slot, g, c].astype(f32)

    def lead_stage(k):
        slot, st = lax.rem(k, IN_SLOTS), lax.rem(k, SEND_SLOTS)
        wait_bytes(own.at[slot], own_sem.at[slot])
        wait_bytes(peer.at[slot], peer_send.at[slot])
        wait_bytes(peer.at[slot], peer_recv.at[slot])

        @pl.when(k >= SEND_SLOTS)
        def _():
            wait_bytes(lead.at[st], lead_send.at[st])

        for role, step in ((0, 2), (1, -1)):
            for g in range(GROUPS):
                dest = at(first(g), step * SIGNS[g])
                for o in range(RING):
                    lead[st, role, g, o] = pair(slot, g, dest, o)
            for g in range(GROUPS):
                into, toward = ((r1, SIGNS[g]), (r2, -SIGNS[g]))[role]
                remote(lead.at[st, role, g], into.at[k, g], lead_send.at[st], r_recv.at[role, k], near_first(g, toward)).start()

    def forward_stage(k):
        slot = lax.rem(k, IN_SLOTS)
        wait_bytes(r1.at[k], r_recv.at[0, k])
        for g in range(GROUPS):
            dest = at(first(g), SIGNS[g])
            for o in range(RING):
                r1[k, g, o] = r1[k, g, o] + pair(slot, g, dest, o)
        for g in range(GROUPS):
            remote(r1.at[k, g], r3.at[k, g], fwd_send.at[k], r_recv.at[2, k], near_first(g, SIGNS[g])).start()

    def part_stage(k):
        slot = lax.rem(k, IN_SLOTS)
        wait_bytes(r2.at[k], r_recv.at[1, k])
        wait_bytes(r3.at[k], r_recv.at[2, k])
        for g in range(GROUPS):
            for o in range(RING):
                r3[k, g, o] = (r3[k, g, o] + r2[k, g, o]) + pair(slot, g, first(g), o)

        @pl.when(k + IN_SLOTS < chunks)
        def _():
            pl.semaphore_signal(peer_free, inc=1, device_id={'data': buddy}, device_id_type=MESH)

        for g in range(GROUPS):
            s = SIGNS[g]
            remote(r3.at[k, g, at(second(g), 2 * s)], p1.at[k, g], part_send.at[k], p_recv.at[0, k], near_second(g, s)).start()
            remote(r3.at[k, g, at(second(g), -s)], p2.at[k, g], part_send.at[k], p_recv.at[1, k], near_second(g, -s)).start()

    def last_stage(k):
        wait_bytes(p1.at[k], p_recv.at[0, k])
        for g in range(GROUPS):
            dest = at(second(g), SIGNS[g])
            p1[k, g] = p1[k, g] + r3[k, g, dest]
        for g in range(GROUPS):
            remote(p1.at[k, g], p3.at[k, g], last_send.at[k], p_recv.at[2, k], near_second(g, SIGNS[g])).start()

    def final_stage(k):
        @pl.when(k == 0)
        def _():
            wait_bytes(mom, mom_sem)

        wait_bytes(p2.at[k], p_recv.at[1, k])
        wait_bytes(p3.at[k], p_recv.at[2, k])
        for g in range(GROUPS):
            j = k * m + g
            total = r3[k, g, second(g)] + p2[k, g] + p3[k, g]
            new = MOMENTUM_COEF * mom[j] + total
            mom[j] = new
            short = new.astype(bf16)
            sq = jnp.sum(new * new, axis=0, keepdims=True)
            sq = functools.reduce(jnp.add, [sq[:, n * 128:(n + 1) * 128] for n in range(cols // 128)])
            half_out[j] = short
            sq_out[j] = sq

            @pl.when(owner_of(k, g) == me)
            def _():
                half_in[k // per_slot, me] = short
                sq_in[k // per_slot, me] = sq

        for g in range(GROUPS):
            j, slot, owner = k * m + g, k // per_slot, owner_of(k, g)

            @pl.when(owner != me)
            def _():
                remote(half_out.at[j], half_in.at[slot, me], half_send, half_recv.at[slot], owner).start()
                remote(sq_out.at[j], sq_in.at[slot, me], sq_send, sq_recv.at[slot], owner).start()

        pltpu.make_async_copy(mom.at[pl.ds(k * m, m)], mom_out.at[pl.ds(k * m, m)], mom_done).start()

    def ns_start(slot):
        wait_bytes(half_in.at[slot, pl.ds(0, devs - 1)], half_recv.at[slot])
        wait_bytes(sq_in.at[slot, pl.ds(0, devs - 1)], sq_recv.at[slot])
        sq = jnp.sum(jnp.sum(sq_in[slot], axis=0), axis=1, keepdims=True)
        scale = jnp.sqrt(sq) + NORM_EPS

        @pl.loop(0, devs)
        def _(d):
            x_buf[slot, pl.ds(pl.multiple_of(d * rows, rows), rows), :] = (half_in[slot, d].astype(f32) / scale).astype(bf16)

    def ns_iter(slot):
        x = x_buf[slot]
        gram[...] = lax.dot_general(x, x, (((1,), (1,)), ((), ())), preferred_element_type=f32).astype(bf16)
        a = gram[...]
        poly[...] = (COEF_B * a.astype(f32) + COEF_C * jnp.dot(a, a, preferred_element_type=f32)).astype(bf16)
        x_buf[slot] = (COEF_A * x.astype(f32) + jnp.dot(poly[...], x, preferred_element_type=f32)).astype(bf16)

    def x_block(slot, d):
        return x_buf.at[slot, pl.ds(pl.multiple_of(d * rows, rows), rows), :]

    def x_give(slot, part):
        j = mine(slot)
        recv = x_recv0 if slot == 0 else x_recv.at[slot - 1, my_turn]
        for dx in range(RING):
            for c in range(CORES):
                d = (lax.rem(py + dx + part, RING) * RING + lax.rem(px + dx, RING)) * CORES + c

                @pl.when(d != me)
                def _():
                    remote(x_block(slot, d), x_in.at[j], x_send.at[slot], recv, d).start()

    def x_keep(slot):
        x_in[mine(slot)] = x_buf[slot, pl.ds(pl.multiple_of(me * rows, rows), rows), :]

    def update(k):
        for g in range(GROUPS):
            j = k * m + g
            old = w[j]
            w[j] = old - LEARN_RATE * (x_in[j].astype(f32) * rms_scale + WEIGHT_DECAY * old)
        pltpu.make_async_copy(w.at[pl.ds(k * m, m)], w_out.at[pl.ds(k * m, m)], w_done).start()

    for k in range(AHEAD):
        fetch_own(jnp.int32(k))
    barrier = pltpu.get_barrier_semaphore()
    near = (buddy, device(at(px, 1), py), device(at(px, -1), py), device(px, at(py, 1)), device(px, at(py, -1)))
    for d in near:
        pl.semaphore_signal(barrier, inc=1, device_id={'data': d}, device_id_type=MESH)
    pl.semaphore_wait(barrier, len(near))
    for k in range(AHEAD):
        fetch_peer(jnp.int32(k))
    pltpu.make_async_copy(mom_in, mom, mom_sem).start()
    pltpu.make_async_copy(w_in, w, w_sem).start()

    drain = chunks
    ended = chunks + 4

    @pl.loop(0, ended + NS_ITERS)
    def _(t):
        @pl.when(t + AHEAD < chunks)
        def _():
            fetch_own(t + AHEAD)
            fetch_peer(t + AHEAD)

        for lag, stage in enumerate((lead_stage, forward_stage, part_stage, last_stage, final_stage)):
            @pl.when(jnp.logical_and(t >= lag, t < chunks + lag))
            def _():
                stage(t - lag)

        for slot in range(slots):
            begin = slot * per_slot + my_turn + 5

            @pl.when(t == begin)
            def _():
                ns_start(slot)

            @pl.when(jnp.logical_and(t >= begin, t < begin + NS_ITERS))
            def _():
                ns_iter(slot)

            @pl.when(t == begin + NS_ITERS - 1)
            def _():
                x_keep(slot)

            if slot < slots - 1:
                @pl.when(jnp.logical_and(t >= drain, t < drain + RING))
                def _():
                    x_give(slot, t - drain)
            else:
                @pl.when(t == jnp.maximum(begin + NS_ITERS - 1, ended))
                def _():
                    @pl.loop(0, RING)
                    def _(part):
                        x_give(slot, part)

    wait_bytes(w, w_sem)
    wait_bytes(half_in.at[0, pl.ds(0, devs - 1)], x_recv0)

    @pl.loop(0, per_slot)
    def _(k):
        update(k)

    @pl.loop(0, per_slot)
    def _(turn):
        @pl.when(turn == my_turn)
        def _():
            wait_bytes(x_in.at[pl.ds(0, m - 1)], x_recv.at[0, turn])

        @pl.when(turn != my_turn)
        def _():
            wait_bytes(x_in.at[pl.ds(0, m)], x_recv.at[0, turn])

        update(per_slot + turn)

    @pl.loop(0, chunks)
    def _(k):
        wait_bytes(r1.at[k], fwd_send.at[k])
        wait_bytes(p1.at[k], part_send.at[k])
        wait_bytes(p2.at[k], part_send.at[k])
        wait_bytes(p1.at[k], last_send.at[k])

    for st in range(SEND_SLOTS):
        wait_bytes(lead.at[st], lead_send.at[st])
    wait_bytes(half_out.at[pl.ds(0, n_mats - slots)], half_send)
    wait_bytes(sq_out.at[pl.ds(0, n_mats - slots)], sq_send)
    for slot in range(slots):
        wait_bytes(half_in.at[slot, pl.ds(0, devs - 1)], x_send.at[slot])
    wait_bytes(mom, mom_done)
    wait_bytes(w, w_done)


def muon(devs, grads, mom, w):
    n_mats, rows, cols = mom.shape
    n_rows = rows * devs
    chips = devs // CORES
    m = GROUPS
    chunks = n_mats // m
    slots = n_mats // devs
    f32, bf16 = jnp.float32, jnp.bfloat16
    dma, vmem = pltpu.SemaphoreType.DMA, pltpu.VMEM
    grads = grads.reshape(n_mats, chips, CORES, rows, cols)
    wide = (chunks, GROUPS, RING, rows, cols)
    thin = (chunks, GROUPS, rows, cols)
    return pl.pallas_call(
        functools.partial(_kernel, devs),
        out_shape=(
            jax.ShapeDtypeStruct(mom.shape, f32),
            jax.ShapeDtypeStruct(w.shape, f32),
        ),
        in_specs=[pl.BlockSpec(memory_space=pl.ANY)] * 3,
        out_specs=(pl.BlockSpec(memory_space=pl.ANY),) * 2,
        scratch_shapes=[
            vmem((IN_SLOTS, m, chips, rows, cols), bf16),
            vmem((IN_SLOTS, m, chips, rows, cols), bf16),
            vmem(wide, f32), vmem(wide, f32), vmem(wide, f32),
            vmem(thin, f32), vmem(thin, f32), vmem(thin, f32),
            vmem((SEND_SLOTS, 2, GROUPS, RING, rows, cols), f32),
            vmem(mom.shape, f32),
            vmem(w.shape, f32),
            vmem(mom.shape, bf16),
            vmem((n_mats, 1, 128), f32),
            vmem((slots, devs, rows, cols), bf16),
            vmem((slots, devs, 1, 128), f32),
            vmem((slots, n_rows, cols), bf16),
            vmem(mom.shape, bf16),
            vmem((n_rows, n_rows), bf16),
            vmem((n_rows, n_rows), bf16),
            dma((IN_SLOTS,)), dma((IN_SLOTS,)), dma((IN_SLOTS,)), pltpu.SemaphoreType.REGULAR,
            dma((SEND_SLOTS,)), dma((3, chunks)), dma((chunks,)), dma((3, chunks)), dma((chunks,)), dma((chunks,)),
            dma, dma, dma, dma, dma, dma, dma((slots,)), dma((slots,)), dma((slots,)), dma, dma((slots - 1, chunks // slots)),
        ],
        compiler_params=pltpu.CompilerParams(
            collective_id=0, has_side_effects=True, vmem_limit_bytes=67043328),
    )(grads, mom, w)


def solution(mesh):
    devs = mesh.shape['data']
    row_spec = P('stage', 'data', None)
    grad_spec = P(('stage', 'data'), None, None, None)

    def local_step(w_rows, mom_rows, grad_full):
        n_mats, rows_dev, n_cols = w_rows.shape
        assert devs == RING * RING * CORES and n_mats == 2 * devs and rows_dev * devs <= n_cols
        mom_new, w_new = muon(devs, grad_full[0], mom_rows, w_rows)
        return w_new, mom_new

    return jax.shard_map(local_step, mesh=mesh, in_specs=(row_spec, row_spec, grad_spec), out_specs=(row_spec, row_spec), check_vma=False)
```

time: 228 us -> 223 us (0.978)
  Pallas kernels: 222 us -> 218 us
  other arithmetic: 3.86 us -> 0 us
  local copies, waits for them, and re-layouts: 1.32 us -> 4.69 us
    pallas_call x1, Pallas kernels: 222 us -> 218 us  [muon(): pl.pallas_call(functools.partial(_kernel, devs), out_shape=(jax.ShapeDtyp...]
    sub x1 -> x0, other arithmetic: 3.86 us -> none  [local_step(): w_rows - LEARN_RATE * (x_rows.astype(jnp.float32) * rms_scale + WEIGHT_DE...]
    unnamed x3 -> x4, local copies, waits for them, and re-layouts: 1.32 us -> 4.69 us
where the time goes in v2:
time: 223 us
  Pallas kernels  218 us (98%)
  local copies, waits for them, and re-layouts  4.69 us (2%)
    pallas_call x1, Pallas kernels, muon(): pl.pallas_call(functools.partial(_kernel, devs), out_shape=(jax.ShapeDtyp...  218 us
    unnamed x4, local copies, waits for them, and re-layouts  4.69 us

profile of v2, /device:TPU:97, one launch (start us, length us, event | category | flops | bytes accessed | tf_op | source)
XLA Modules:
  0.0 223.2 jit_solution(5214320231801017317)
XLA Ops:
  0.6 217.8 %shard_map.50 = (f32[64,16,512]{2,1,0:T(8,128)}, f32[64,16,512]{2,1,0:T(8,128)}) custom-call(bf16[64,16,2,16,512]{4,3,2,1,0:T(8,128)(2,1)} %bitcast.1, f32[64,16,512]{2,1,0:T(8,128)} %mom_in.1, f32[64,16,512]{2,1,0:T(8,128)} %w_in.1), custom_call_target="tpu_custom_call" | custom-call | tf_op jit(solution)/shard_map/pallas_call | solution.py:336
  218.5 0.0 copy-start
  218.5 3.4 %copy.7 = f32[64,16,512]{2,1,0:T(8,128)} copy(f32[64,16,512]{2,1,0:T(8,128)} %get-tuple-element.8) | data formatting | bytes 4194304
  221.9 0.0 copy-done
  221.9 1.3 copy.8
Async XLA Ops:
  218.5 3.4 %copy-start = (f32[64,16,512]{2,1,0:T(8,128)S(1)}, f32[64,16,512]{2,1,0:T(8,128)}, u32[]{:S(2)}) copy-start(f32[64,16,512]{2,1,0:T(8,128)} %get-tuple-element.9) | copy-start | bytes 6291460

commit v3 on v2

v3 whole, which is shorter than its diff:
```python
import functools
import math

import jax
import jax.numpy as jnp
from jax import lax
from jax.experimental import pallas as pl
from jax.experimental.pallas import tpu as pltpu
from jax.sharding import PartitionSpec as P

MOMENTUM_COEF = 0.95
LEARN_RATE = 0.05
WEIGHT_DECAY = 0.2
NORM_EPS = 1e-7
COEF_A = 3.4445
COEF_B = -4.7750
COEF_C = 2.0315
NS_ITERS = 5
EARLY = 3

CORES = 2
RING = 4
SIGNS = (1, -1, 1, -1)
X_FIRST = (True, True, False, False)
GROUPS = 4
IN_SLOTS = 6
SEND_SLOTS = 3
AHEAD = 2
MESH = pl.DeviceIdType.MESH


def _kernel(
    devs, grads, mom_in, w_in, mom, w,
    own, peer, r1, r2, r3, p1, p2, p3, lead, raw, half_out, sq_out, half_in, sq_in, x_buf, x_in, gram, poly,
    own_sem, peer_send, peer_recv, peer_free, lead_send, raw_send, r_recv, fwd_send, p_recv, part_send, last_send,
    mom_sem, w_sem, half_send, sq_send, half_recv, sq_recv, x_send, x_recv0, x_recv,
):
    n_mats, rows, cols = mom.shape
    m = GROUPS
    chunks = n_mats // m
    slots = n_mats // devs
    per_slot = chunks // slots
    rms_scale = 0.2 * math.sqrt(max(rows * devs, cols))
    f32, bf16 = jnp.float32, jnp.bfloat16

    me = lax.axis_index('data')
    core = lax.rem(me, CORES)
    chip = me // CORES
    px, py = lax.rem(chip, RING), chip // RING
    buddy = me + 1 - 2 * core

    def at(pos, step):
        return lax.rem(pos + step + RING, RING)

    def device(x, y):
        return (y * RING + x) * CORES + core

    def first(g):
        return px if X_FIRST[g] else py

    def second(g):
        return py if X_FIRST[g] else px

    def near_first(g, step):
        return device(at(px, step), py) if X_FIRST[g] else device(px, at(py, step))

    def near_second(g, step):
        return device(px, at(py, step)) if X_FIRST[g] else device(at(px, step), py)

    def remote(src, dst, send, recv, target):
        return pltpu.make_async_remote_copy(
            src_ref=src, dst_ref=dst, send_sem=send, recv_sem=recv,
            device_id={'data': target}, device_id_type=MESH)

    def wait_bytes(ref, sem):
        pltpu.make_async_copy(ref, ref, sem).wait()

    def owner_of(k, g):
        kk = lax.rem(k, per_slot)
        return (g * RING + lax.rem(kk + g, RING)) * CORES + kk // RING

    my_turn = RING * core + at(px, -py)

    def mine(slot):
        return (slot * per_slot + my_turn) * m + py

    def fetch_own(k):
        slot = lax.rem(k, IN_SLOTS)
        pltpu.make_async_copy(grads.at[pl.ds(k * m, m), :, :, core], own.at[slot], own_sem.at[slot]).start()

    def fetch_peer(k):
        slot = lax.rem(k, IN_SLOTS)

        @pl.when(k >= IN_SLOTS)
        def _():
            pl.semaphore_wait(peer_free, 1)

        remote(grads.at[pl.ds(k * m, m), :, :, 1 - core], peer.at[slot], peer_send.at[slot], peer_recv.at[slot], buddy).start()

    def pair(slot, g, on_first, o):
        y, x = (o, on_first) if X_FIRST[g] else (on_first, o)
        return own[slot, g, y, x].astype(f32) + peer[slot, g, y, x].astype(f32)

    def lead_stage(k):
        slot, st = lax.rem(k, IN_SLOTS), lax.rem(k, SEND_SLOTS)
        wait_bytes(own.at[slot], own_sem.at[slot])
        wait_bytes(peer.at[slot], peer_send.at[slot])
        wait_bytes(peer.at[slot], peer_recv.at[slot])

        @pl.when(k > SEND_SLOTS)
        def _():
            wait_bytes(lead.at[st], lead_send.at[st])

        @pl.when(k > 0)
        def _():
            for role, step in ((0, 2), (1, -1)):
                for g in range(GROUPS):
                    dest = at(first(g), step * SIGNS[g])
                    for o in range(RING):
                        lead[st, role, g, o] = pair(slot, g, dest, o)
                for g in range(GROUPS):
                    into, toward = ((r1, SIGNS[g]), (r2, -SIGNS[g]))[role]
                    remote(lead.at[st, role, g], into.at[k, g], lead_send.at[st], r_recv.at[role, k], near_first(g, toward)).start()

    def raw_leads():
        for role, step in ((0, 2), (1, -1)):
            for g in range(GROUPS):
                dest = at(first(g), step * SIGNS[g])
                toward = near_first(g, (SIGNS[g], -SIGNS[g])[role])
                for c in (core, 1 - core):
                    block = grads.at[g, :, dest, c] if X_FIRST[g] else grads.at[g, dest, :, c]
                    target = toward - core + c
                    remote(block, raw.at[role, g, core], raw_send, r_recv.at[role, 0], target).start()

    def raw_pair(role, g, o):
        return raw[role, g, 0, o].astype(f32) + raw[role, g, 1, o].astype(f32)

    def forward_stage(k):
        slot = lax.rem(k, IN_SLOTS)

        @pl.when(k == 0)
        def _():
            wait_bytes(raw.at[0], r_recv.at[0, 0])
            for g in range(GROUPS):
                dest = at(first(g), SIGNS[g])
                for o in range(RING):
                    r1[0, g, o] = raw_pair(0, g, o) + pair(0, g, dest, o)

        @pl.when(k > 0)
        def _():
            wait_bytes(r1.at[k], r_recv.at[0, k])
            for g in range(GROUPS):
                dest = at(first(g), SIGNS[g])
                for o in range(RING):
                    r1[k, g, o] = r1[k, g, o] + pair(slot, g, dest, o)

        for g in range(GROUPS):
            remote(r1.at[k, g], r3.at[k, g], fwd_send.at[k], r_recv.at[2, k], near_first(g, SIGNS[g])).start()

    def part_stage(k):
        slot = lax.rem(k, IN_SLOTS)
        wait_bytes(r3.at[k], r_recv.at[2, k])

        @pl.when(k == 0)
        def _():
            wait_bytes(raw.at[1], r_recv.at[1, 0])
            for g in range(GROUPS):
                for o in range(RING):
                    r3[0, g, o] = (r3[0, g, o] + raw_pair(1, g, o)) + pair(0, g, first(g), o)

        @pl.when(k > 0)
        def _():
            wait_bytes(r2.at[k], r_recv.at[1, k])
            for g in range(GROUPS):
                for o in range(RING):
                    r3[k, g, o] = (r3[k, g, o] + r2[k, g, o]) + pair(slot, g, first(g), o)


        @pl.when(k + IN_SLOTS < chunks)
        def _():
            pl.semaphore_signal(peer_free, inc=1, device_id={'data': buddy}, device_id_type=MESH)

        straight = k == chunks - 1
        for g in range(GROUPS):
            s = SIGNS[g]
            far = near_second(g, jnp.where(straight, 2 * s, s))
            remote(r3.at[k, g, at(second(g), 2 * s)], p1.at[k, g], part_send.at[k], p_recv.at[0, k], far).start()
            remote(r3.at[k, g, at(second(g), -s)], p2.at[k, g], part_send.at[k], p_recv.at[1, k], near_second(g, -s)).start()

            @pl.when(straight)
            def _():
                remote(r3.at[k, g, at(second(g), s)], p3.at[k, g], last_send.at[k], p_recv.at[2, k], near_second(g, s)).start()

    def last_stage(k):
        wait_bytes(p1.at[k], p_recv.at[0, k])

        @pl.when(k < chunks - 1)
        def _():
            for g in range(GROUPS):
                dest = at(second(g), SIGNS[g])
                p1[k, g] = p1[k, g] + r3[k, g, dest]
            for g in range(GROUPS):
                remote(p1.at[k, g], p3.at[k, g], last_send.at[k], p_recv.at[2, k], near_second(g, SIGNS[g])).start()

        @pl.when(k == chunks - 1)
        def _():
            for g in range(GROUPS):
                r3[k, g, second(g)] = r3[k, g, second(g)] + p1[k, g]

    def give(k):
        for g in range(GROUPS):
            j, slot, owner = k * m + g, k // per_slot, owner_of(k, g)

            @pl.when(owner != me)
            def _():
                remote(half_out.at[j], half_in.at[slot, me], half_send, half_recv.at[slot], owner).start()
                remote(sq_out.at[j], sq_in.at[slot, me], sq_send, sq_recv.at[slot], owner).start()

    def final_stage(k):
        @pl.when(k == 0)
        def _():
            wait_bytes(mom, mom_sem)

        wait_bytes(p2.at[k], p_recv.at[1, k])
        wait_bytes(p3.at[k], p_recv.at[2, k])
        for g in range(GROUPS):
            j = k * m + g
            total = r3[k, g, second(g)] + p2[k, g] + p3[k, g]
            new = MOMENTUM_COEF * mom[j] + total
            mom[j] = new
            short = new.astype(bf16)
            sq = jnp.sum(new * new, axis=0, keepdims=True)
            sq = functools.reduce(jnp.add, [sq[:, n * 128:(n + 1) * 128] for n in range(cols // 128)])
            half_out[j] = short
            sq_out[j] = sq

            @pl.when(owner_of(k, g) == me)
            def _():
                half_in[k // per_slot, me] = short
                sq_in[k // per_slot, me] = sq

        @pl.when(k < chunks - RING)
        def _():
            give(k)

        @pl.when(k == chunks - 1)
        def _():
            @pl.loop(chunks - RING, chunks)
            def _(late):
                give(late)

    def ns_start(slot):
        wait_bytes(half_in.at[slot, pl.ds(0, devs - 1)], half_recv.at[slot])
        wait_bytes(sq_in.at[slot, pl.ds(0, devs - 1)], sq_recv.at[slot])
        sq = jnp.sum(jnp.sum(sq_in[slot], axis=0), axis=1, keepdims=True)
        scale = jnp.sqrt(sq) + NORM_EPS

        @pl.loop(0, devs)
        def _(d):
            x_buf[slot, pl.ds(pl.multiple_of(d * rows, rows), rows), :] = (half_in[slot, d].astype(f32) / scale).astype(bf16)

    def ns_iter(slot):
        x = x_buf[slot]
        gram[...] = lax.dot_general(x, x, (((1,), (1,)), ((), ())), preferred_element_type=f32).astype(bf16)
        a = gram[...]
        poly[...] = (COEF_B * a.astype(f32) + COEF_C * jnp.dot(a, a, preferred_element_type=f32)).astype(bf16)
        x_buf[slot] = (COEF_A * x.astype(f32) + jnp.dot(poly[...], x, preferred_element_type=f32)).astype(bf16)

    def ns_iters(slot, lo, hi):
        @pl.loop(lo, hi)
        def _(_):
            ns_iter(slot)

    def x_block(slot, d):
        return x_buf.at[slot, pl.ds(pl.multiple_of(d * rows, rows), rows), :]

    def x_give(slot, part):
        j = mine(slot)
        recv = x_recv0 if slot == 0 else x_recv.at[slot - 1, my_turn]
        for dx in range(RING):
            for c in range(CORES):
                d = (lax.rem(py + dx + part, RING) * RING + lax.rem(px + dx, RING)) * CORES + c

                @pl.when(d != me)
                def _():
                    remote(x_block(slot, d), x_in.at[j], x_send.at[slot], recv, d).start()

    def x_give_all(slot):
        @pl.loop(0, RING)
        def _(part):
            x_give(slot, part)

    def x_keep(slot):
        x_in[mine(slot)] = x_buf[slot, pl.ds(pl.multiple_of(me * rows, rows), rows), :]

    def update(k):
        for g in range(GROUPS):
            j = k * m + g
            old = w[j]
            w[j] = old - LEARN_RATE * (x_in[j].astype(f32) * rms_scale + WEIGHT_DECAY * old)

    for k in range(AHEAD):
        fetch_own(jnp.int32(k))
    barrier = pltpu.get_barrier_semaphore()
    near = (buddy, device(at(px, 1), py), device(at(px, -1), py), device(px, at(py, 1)), device(px, at(py, -1)))
    near += tuple(d - core + 1 - core for d in near[1:])
    for d in near:
        pl.semaphore_signal(barrier, inc=1, device_id={'data': d}, device_id_type=MESH)
    pl.semaphore_wait(barrier, len(near))
    raw_leads()
    for k in range(AHEAD):
        fetch_peer(jnp.int32(k))
    pltpu.make_async_copy(mom_in, mom, mom_sem).start()
    pltpu.make_async_copy(w_in, w, w_sem).start()

    @pl.loop(0, chunks + 4)
    def _(t):
        @pl.when(t + AHEAD < chunks)
        def _():
            fetch_own(t + AHEAD)
            fetch_peer(t + AHEAD)

        for lag, stage in enumerate((lead_stage, forward_stage, part_stage, last_stage, final_stage)):
            @pl.when(jnp.logical_and(t >= lag, t < chunks + lag))
            def _():
                stage(t - lag)

        for slot in range(slots):
            begin = slot * per_slot + my_turn + 5

            @pl.when(jnp.logical_and(t == begin, begin <= chunks))
            def _():
                ns_start(slot)
                ns_iters(slot, 0, EARLY)

            @pl.when(jnp.logical_and(t == begin + 1, begin < chunks))
            def _():
                ns_iters(slot, EARLY, NS_ITERS)
                x_keep(slot)
    end = slots - 1
    busy = my_turn >= RING

    @pl.when(jnp.logical_not(busy))
    def _():
        x_give_all(0)

        @pl.when(my_turn == RING - 1)
        def _():
            ns_iters(end, EARLY, NS_ITERS)
            x_keep(end)

        x_give_all(end)

    @pl.when(busy)
    def _():
        ns_start(end)
        x_give_all(0)
        ns_iters(end, 0, NS_ITERS)
        x_keep(end)
        x_give_all(end)

    @pl.loop(0, chunks)
    def _(k):
        wait_bytes(r1.at[k], fwd_send.at[k])
        wait_bytes(p1.at[k], part_send.at[k])
        wait_bytes(p2.at[k], part_send.at[k])
        wait_bytes(p1.at[k], last_send.at[k])

    for st in range(SEND_SLOTS):
        wait_bytes(lead.at[st], lead_send.at[st])
    wait_bytes(raw, raw_send)
    wait_bytes(half_out.at[pl.ds(0, n_mats - slots)], half_send)
    wait_bytes(sq_out.at[pl.ds(0, n_mats - slots)], sq_send)
    wait_bytes(w, w_sem)
    wait_bytes(half_in.at[0, pl.ds(0, devs - 1)], x_recv0)

    @pl.loop(0, per_slot)
    def _(k):
        update(k)

    @pl.loop(0, per_slot)
    def _(turn):
        @pl.when(turn == my_turn)
        def _():
            wait_bytes(x_in.at[pl.ds(0, m - 1)], x_recv.at[0, turn])

        @pl.when(turn != my_turn)
        def _():
            wait_bytes(x_in.at[pl.ds(0, m)], x_recv.at[0, turn])

        update(per_slot + turn)

    for slot in range(slots):
        wait_bytes(half_in.at[slot, pl.ds(0, devs - 1)], x_send.at[slot])


def _store(mom, w, mom_out, w_out, sem):
    copies = [pltpu.make_async_copy(a, b, sem.at[n]) for n, (a, b) in enumerate(((mom, mom_out), (w, w_out)))]
    for copy in copies:
        copy.start()
    for copy in copies:
        copy.wait()


def store(mom, w):
    return pl.pallas_call(
        _store,
        out_shape=(jax.ShapeDtypeStruct(mom.shape, mom.dtype), jax.ShapeDtypeStruct(w.shape, w.dtype)),
        in_specs=[pl.BlockSpec(memory_space=pltpu.VMEM)] * 2,
        out_specs=(pl.BlockSpec(memory_space=pl.ANY),) * 2,
        scratch_shapes=[pltpu.SemaphoreType.DMA((2,))],
        compiler_params=pltpu.CompilerParams(vmem_limit_bytes=2**20),
    )(mom, w)


def muon(devs, grads, mom, w):
    n_mats, rows, cols = mom.shape
    n_rows = rows * devs
    m = GROUPS
    chunks = n_mats // m
    slots = n_mats // devs
    f32, bf16 = jnp.float32, jnp.bfloat16
    dma, vmem = pltpu.SemaphoreType.DMA, pltpu.VMEM
    grads = grads.reshape(n_mats, RING, RING, CORES, rows, cols)
    wide = (chunks, GROUPS, RING, rows, cols)
    thin = (chunks, GROUPS, rows, cols)
    return pl.pallas_call(
        functools.partial(_kernel, devs),
        out_shape=(
            vmem(mom.shape, f32),
            vmem(w.shape, f32),
        ),
        in_specs=[pl.BlockSpec(memory_space=pl.ANY)] * 3,
        out_specs=(pl.BlockSpec(memory_space=vmem),) * 2,
        scratch_shapes=[
            vmem((IN_SLOTS, m, RING, RING, rows, cols), bf16),
            vmem((IN_SLOTS, m, RING, RING, rows, cols), bf16),
            vmem(wide, f32), vmem(wide, f32), vmem(wide, f32),
            vmem(thin, f32), vmem(thin, f32), vmem(thin, f32),
            vmem((SEND_SLOTS, 2, GROUPS, RING, rows, cols), f32),
            vmem((2, GROUPS, CORES, RING, rows, cols), bf16),
            vmem(mom.shape, bf16),
            vmem((n_mats, 1, 128), f32),
            vmem((slots, devs, rows, cols), bf16),
            vmem((slots, devs, 1, 128), f32),
            vmem((slots, n_rows, cols), bf16),
            vmem(mom.shape, bf16),
            vmem((n_rows, n_rows), bf16),
            vmem((n_rows, n_rows), bf16),
            dma((IN_SLOTS,)), dma((IN_SLOTS,)), dma((IN_SLOTS,)), pltpu.SemaphoreType.REGULAR,
            dma((SEND_SLOTS,)), dma, dma((3, chunks)), dma((chunks,)), dma((3, chunks)), dma((chunks,)), dma((chunks,)),
            dma, dma, dma, dma, dma((slots,)), dma((slots,)), dma((slots,)), dma, dma((slots - 1, chunks // slots)),
        ],
        compiler_params=pltpu.CompilerParams(
            collective_id=0, has_side_effects=True, vmem_limit_bytes=57 * 2**20),
    )(grads, mom, w)


def solution(mesh):
    devs = mesh.shape['data']
    row_spec = P('stage', 'data', None)
    grad_spec = P(('stage', 'data'), None, None, None)

    def local_step(w_rows, mom_rows, grad_full):
        n_mats, rows_dev, n_cols = w_rows.shape
        assert devs == RING * RING * CORES and n_mats == 2 * devs and rows_dev * devs <= n_cols
        mom_new, w_new = store(*muon(devs, grad_full[0], mom_rows, w_rows))
        return w_new, mom_new

    return jax.shard_map(local_step, mesh=mesh, in_specs=(row_spec, row_spec, grad_spec), out_specs=(row_spec, row_spec), check_vma=False)
```

time: 223 us -> 213 us (0.955)
  Pallas kernels: 218 us -> 213 us
  local copies, waits for them, and re-layouts: 4.69 us -> 0 us
    pallas_call x1 -> x2, Pallas kernels: 218 us -> 213 us  [the longest x1 211 us: muon(): pl.pallas_call(functools.partial(_kernel, devs), out_shape=(vmem(mom.shap...]
    unnamed x4 -> x0, local copies, waits for them, and re-layouts: 4.69 us -> none
where the time goes in v3:
time: 213 us
  Pallas kernels  213 us (100%)
    pallas_call x1, Pallas kernels, muon(): pl.pallas_call(functools.partial(_kernel, devs), out_shape=(vmem(mom.shap...  211 us

profile of v3, /device:TPU:97, one launch (start us, length us, event | category | flops | bytes accessed | tf_op | source)
XLA Modules:
  0.0 213.4 jit_solution(11613184656675244321)
XLA Ops:
  0.6 210.7 %shard_map.50 = (f32[64,16,512]{2,1,0:T(8,128)S(1)}, f32[64,16,512]{2,1,0:T(8,128)S(1)}) custom-call(bf16[64,4,4,2,16,512]{5,4,3,2,1,0:T(8,128)(2,1)} %bitcast.1, f32[64,16,512]{2,1,0:T(8,128)} %mom_in.1, f32[64,16,512]{2,1,0:T(8,128)} %w_in.1), custom_call_target="tpu_custom_call" | custom-call | tf_op jit(solution)/shard_map/pallas_call | solution.py:427
  211.3 2.0 shard_map.51

commit v4 on v3

--- a/solution.py
+++ b/solution.py
@@ -27,6 +27,9 @@
 SEND_SLOTS = 3
 AHEAD = 2
 MESH = pl.DeviceIdType.MESH
+TRIPS = sorted(
+    ((x, y, c) for x in range(RING) for y in range(RING) for c in range(CORES) if x or y or c),
+    key=lambda t: -min(t[0], RING - t[0]) - min(t[1], RING - t[1]))
 
 
 def _kernel(
@@ -239,9 +242,15 @@
                 half_in[k // per_slot, me] = short
                 sq_in[k // per_slot, me] = sq
 
-        @pl.when(k < chunks - RING)
+        @pl.when(k < per_slot)
         def _():
             give(k)
+
+        @pl.when(k == chunks - 3)
+        def _():
+            @pl.loop(per_slot, chunks - RING)
+            def _(late):
+                give(late)
 
         @pl.when(k == chunks - 1)
         def _():
@@ -274,21 +283,13 @@
     def x_block(slot, d):
         return x_buf.at[slot, pl.ds(pl.multiple_of(d * rows, rows), rows), :]
 
-    def x_give(slot, part):
+    def x_give(slot, trips):
         j = mine(slot)
         recv = x_recv0 if slot == 0 else x_recv.at[slot - 1, my_turn]
-        for dx in range(RING):
-            for c in range(CORES):
-                d = (lax.rem(py + dx + part, RING) * RING + lax.rem(px + dx, RING)) * CORES + c
-
-                @pl.when(d != me)
-                def _():
-                    remote(x_block(slot, d), x_in.at[j], x_send.at[slot], recv, d).start()
-
-    def x_give_all(slot):
-        @pl.loop(0, RING)
-        def _(part):
-            x_give(slot, part)
+        for dx, dy, other in trips:
+            c = 1 - core if other else core
+            d = (at(py, dy) * RING + at(px, dx)) * CORES + c
+            remote(x_block(slot, d), x_in.at[j], x_send.at[slot], recv, d).start()
 
     def x_keep(slot):
         x_in[mine(slot)] = x_buf[slot, pl.ds(pl.multiple_of(me * rows, rows), rows), :]
@@ -325,39 +326,25 @@
             def _():
                 stage(t - lag)
 
-        for slot in range(slots):
-            begin = slot * per_slot + my_turn + 5
-
-            @pl.when(jnp.logical_and(t == begin, begin <= chunks))
-            def _():
-                ns_start(slot)
-                ns_iters(slot, 0, EARLY)
-
-            @pl.when(jnp.logical_and(t == begin + 1, begin < chunks))
-            def _():
-                ns_iters(slot, EARLY, NS_ITERS)
-                x_keep(slot)
+        begin = my_turn + 5
+
+        @pl.when(t == begin)
+        def _():
+            ns_start(0)
+            ns_iters(0, 0, EARLY)
+
+        @pl.when(t == begin + 1)
+        def _():
+            ns_iters(0, EARLY, NS_ITERS)
+            x_keep(0)
+
     end = slots - 1
-    busy = my_turn >= RING
-
-    @pl.when(jnp.logical_not(busy))
-    def _():
-        x_give_all(0)
-
-        @pl.when(my_turn == RING - 1)
-        def _():
-            ns_iters(end, EARLY, NS_ITERS)
-            x_keep(end)
-
-        x_give_all(end)
-
-    @pl.when(busy)
-    def _():
-        ns_start(end)
-        x_give_all(0)
-        ns_iters(end, 0, NS_ITERS)
-        x_keep(end)
-        x_give_all(end)
+    ns_start(end)
+    for i in range(NS_ITERS):
+        x_give(0, TRIPS[i::NS_ITERS])
+        ns_iter(end)
+    x_keep(end)
+    x_give(end, TRIPS)
 
     @pl.loop(0, chunks)
     def _(k):

time: 213 us -> 212 us (level)
  no operation moved by 1% of the time
where the time goes in v4:
time: 212 us
  Pallas kernels  211 us (100%)
    pallas_call x1, Pallas kernels, muon(): pl.pallas_call(functools.partial(_kernel, devs), out_shape=(vmem(mom.shap...  209 us

profile of v4, /device:TPU:97, one launch (start us, length us, event | category | flops | bytes accessed | tf_op | source)
XLA Modules:
  0.0 211.6 jit_solution(4367796324509515449)
XLA Ops:
  0.6 208.9 %shard_map.50 = (f32[64,16,512]{2,1,0:T(8,128)S(1)}, f32[64,16,512]{2,1,0:T(8,128)S(1)}) custom-call(bf16[64,4,4,2,16,512]{5,4,3,2,1,0:T(8,128)(2,1)} %bitcast.1, f32[64,16,512]{2,1,0:T(8,128)} %mom_in.1, f32[64,16,512]{2,1,0:T(8,128)} %w_in.1), custom_call_target="tpu_custom_call" | custom-call | tf_op jit(solution)/shard_map/pallas_call | solution.py:414
  209.6 2.0 shard_map.51

commit v5 on v4

--- a/solution.py
+++ b/solution.py
@@ -27,9 +27,10 @@
 SEND_SLOTS = 3
 AHEAD = 2
 MESH = pl.DeviceIdType.MESH
-TRIPS = sorted(
-    ((x, y, c) for x in range(RING) for y in range(RING) for c in range(CORES) if x or y or c),
+WAYS = sorted(
+    ((x, y) for x in range(RING) for y in range(RING)),
     key=lambda t: -min(t[0], RING - t[0]) - min(t[1], RING - t[1]))
+TRIPS = [(x, y, c) for x, y in WAYS for c in range(CORES) if x or y or c]
 
 
 def _kernel(
@@ -219,6 +220,20 @@
                 remote(half_out.at[j], half_in.at[slot, me], half_send, half_recv.at[slot], owner).start()
                 remote(sq_out.at[j], sq_in.at[slot, me], sq_send, sq_recv.at[slot], owner).start()
 
+    def give_block(slot, c):
+        for dx, dy in WAYS:
+            tx, ty = at(px, dx), at(py, dy)
+            j, owner = (slot * per_slot + RING * c + at(tx, -ty)) * m + ty, (ty * RING + tx) * CORES + c
+
+            def send():
+                remote(half_out.at[j], half_in.at[slot, me], half_send, half_recv.at[slot], owner).start()
+                remote(sq_out.at[j], sq_in.at[slot, me], sq_send, sq_recv.at[slot], owner).start()
+
+            if dx or dy:
+                send()
+            else:
+                pl.when(core != c)(send)
+
     def final_stage(k):
         @pl.when(k == 0)
         def _():
@@ -248,15 +263,11 @@
 
         @pl.when(k == chunks - 3)
         def _():
-            @pl.loop(per_slot, chunks - RING)
-            def _(late):
-                give(late)
+            give_block(slots - 1, 0)
 
         @pl.when(k == chunks - 1)
         def _():
-            @pl.loop(chunks - RING, chunks)
-            def _(late):
-                give(late)
+            give_block(slots - 1, 1)
 
     def ns_start(slot):
         wait_bytes(half_in.at[slot, pl.ds(0, devs - 1)], half_recv.at[slot])

time: 212 us -> 211 us (level)
  no operation moved by 1% of the time
where the time goes in v5:
time: 211 us
  Pallas kernels  210 us (100%)
    pallas_call x1, Pallas kernels, muon(): pl.pallas_call(functools.partial(_kernel, devs), out_shape=(vmem(mom.shap...  208 us

profile of v5, /device:TPU:97, one launch (start us, length us, event | category | flops | bytes accessed | tf_op | source)
XLA Modules:
  0.0 210.7 jit_solution(6620801927073713034)
XLA Ops:
  0.6 208.0 %shard_map.50 = (f32[64,16,512]{2,1,0:T(8,128)S(1)}, f32[64,16,512]{2,1,0:T(8,128)S(1)}) custom-call(bf16[64,4,4,2,16,512]{5,4,3,2,1,0:T(8,128)(2,1)} %bitcast.1, f32[64,16,512]{2,1,0:T(8,128)} %mom_in.1, f32[64,16,512]{2,1,0:T(8,128)} %w_in.1), custom_call_target="tpu_custom_call" | custom-call | tf_op jit(solution)/shard_map/pallas_call | solution.py:425
  208.6 2.0 shard_map.51

commit v6 on v5

--- a/solution.py
+++ b/solution.py
@@ -195,6 +195,10 @@
             def _():
                 remote(r3.at[k, g, at(second(g), s)], p3.at[k, g], last_send.at[k], p_recv.at[2, k], near_second(g, s)).start()
 
+        @pl.when(straight)
+        def _():
+            give_block(slots - 1, 0)
+
     def last_stage(k):
         wait_bytes(p1.at[k], p_recv.at[0, k])
 
@@ -260,10 +264,6 @@
         @pl.when(k < per_slot)
         def _():
             give(k)
-
-        @pl.when(k == chunks - 3)
-        def _():
-            give_block(slots - 1, 0)
 
         @pl.when(k == chunks - 1)
         def _():

time: 211 us -> 212 us (level)
  no operation moved by 1% of the time
where the time goes in v6:
time: 212 us
  Pallas kernels  211 us (100%)
    pallas_call x1, Pallas kernels, muon(): pl.pallas_call(functools.partial(_kernel, devs), out_shape=(vmem(mom.shap...  209 us

profile of v6, /device:TPU:97, one launch (start us, length us, event | category | flops | bytes accessed | tf_op | source)
XLA Modules:
  0.0 212.1 jit_solution(2542309825291207909)
XLA Ops:
  0.6 209.4 %shard_map.50 = (f32[64,16,512]{2,1,0:T(8,128)S(1)}, f32[64,16,512]{2,1,0:T(8,128)S(1)}) custom-call(bf16[64,4,4,2,16,512]{5,4,3,2,1,0:T(8,128)(2,1)} %bitcast.1, f32[64,16,512]{2,1,0:T(8,128)} %mom_in.1, f32[64,16,512]{2,1,0:T(8,128)} %w_in.1), custom_call_target="tpu_custom_call" | custom-call | tf_op jit(solution)/shard_map/pallas_call | solution.py:425
  210.0 2.0 shard_map.51
